TPU v7x, 32 devices: a whole 2x2x4 slice. The times are simulated.
32 devices in a mesh: px: 4 (over y, x), py: 8 (over z, core).
Axes of the slice: x: 2, y: 2, z: 4, core: 2. Of those that a mesh axis runs over, the one named last changes fastest.
Arguments:
- white_noise: float32 [2, 64, 256, 256], P(None, 'px', 'py'), may hold values from -6 to 6
- spectrum: float32 [64, 256, 256], P('px', 'py'), may hold values from 0.1 to 2, as said below
- group_table: int32 [3, 8], replicated, may hold values from 0 to 7, each once within a row
Outputs:
- modulus: float32 [2, 64, 256, 256], P(None, 'px', 'py')
- level_one: float32 [2, 32, 128, 128], P(None, 'px', 'py')
- level_two: float32 [2, 16, 64, 64], P(None, 'px', 'py')
- level_three: float32 [2, 8, 32, 32], P(None, 'px', 'py')
Inputs may be any that keep to these rules, and one draw needn't show every extreme that they name: spectrum[j, m, k] equals spectrum[(64 - j) % 64, (256 - m) % 256, (256 - k) % 256]. `group_table`: each row is a permutation of 0 to 7.
All inputs are finite; a program needn't handle non-finite values.
Results may differ from a plain program's by a relative error of at most 0.000088.
Values sent between devices are 32-bit elements; how exact they have to be, the bound alone decides.
A program may use at most 192 MiB of HBM per device.

v0:
```python
import numpy as np
import jax
import jax.numpy as jnp
from jax import lax
from jax.sharding import PartitionSpec as P


def angles_of(length):
    positions = np.arange(length, dtype=np.int64)
    return positions[:, None] * positions[None, :] % length * (2.0 * np.pi / length)


def complex_table(length, direction):
    angles = angles_of(length)
    cos, sin = (np.cos(angles), direction * np.sin(angles))
    table = np.stack([np.stack([cos, sin], 1), np.stack([-sin, cos], 1)], 0)
    return jnp.asarray(table, jnp.float32)


def half_tables(length):
    angles = angles_of(length)[:, : length // 2]
    ahead = np.stack([np.cos(angles), -np.sin(angles)], 1)
    back = 2.0 * ahead
    nyquist = np.where(np.arange(length) % 2 == 0, 1.0, -1.0)
    ahead[:, 1, 0] = nyquist
    back[:, 0, 0] = 1.0
    back[:, 1, 0] = nyquist
    return (jnp.asarray(ahead, jnp.float32), jnp.asarray(back, jnp.float32))


def einsum(pattern, left, right):
    return jnp.einsum(pattern, left, right, precision=lax.Precision.HIGH)


def swap_first(values):
    first = values[:, :, :1]
    turned = jnp.swapaxes(first, 0, 1)
    return jnp.concatenate([turned, values[:, :, 1:]], 2)


def coarsen(values):
    members, size_x, size_y, size_z = values.shape
    blocks = values.reshape(members, size_x // 2, 2, size_y // 2, 2, size_z // 2, 2)
    return blocks.mean(axis=(2, 4, 6))


def on_device(white_noise, spectrum, group_table):
    members, cells_x, cells_y, length_z = white_noise.shape
    size_px, size_py = (lax.axis_size("px"), lax.axis_size("py"))
    length_x, length_y = (cells_x * size_px, cells_y * size_py)
    half_z = length_z // 2
    block_py, block = (half_z // size_py, half_z // size_py // size_px)
    z_ahead, z_back = half_tables(length_z)
    scale = 1.0 / (length_x * length_y * length_z)
    table = jnp.transpose(spectrum, (2, 0, 1))
    last = jnp.broadcast_to(table[half_z : half_z + 1], (size_py, 1, cells_x, cells_y))
    table = jnp.concatenate([table[:half_z].reshape(size_py, block_py, cells_x, cells_y), last], 1)
    table = lax.all_to_all(table, "py", split_axis=0, concat_axis=3, tiled=True)[0]
    last = jnp.broadcast_to(table[block_py:], (size_px, 1, cells_x, length_y))
    table = jnp.concatenate([table[:block_py].reshape(size_px, block, cells_x, length_y), last], 1)
    table = lax.all_to_all(table, "px", split_axis=0, concat_axis=2, tiled=True)[0] * scale
    is_first = (lax.axis_index("px") == 0) & (lax.axis_index("py") == 0)
    other = jnp.where(is_first, table[block:], table[:1])
    tables = jnp.stack([table[:block], jnp.concatenate([other, table[1:block]], 0)], 0)
    values = einsum("fxyz,zck->fckxy", white_noise, z_ahead)
    values = swap_first(values)
    values = lax.all_to_all(values, "py", split_axis=2, concat_axis=4, tiled=True)
    values = einsum("fckxy,cydm->fdkxm", values, complex_table(length_y, -1.0))
    values = lax.all_to_all(values, "px", split_axis=2, concat_axis=3, tiled=True)
    values = einsum("fckxm,cxdj->fdkjm", values, complex_table(length_x, -1.0))
    values = values * tables[:, None]
    values = einsum("fckjm,cjdx->fdkxm", values, complex_table(length_x, 1.0))
    values = lax.all_to_all(values, "px", split_axis=3, concat_axis=2, tiled=True)
    values = einsum("fckxm,cmdy->fdkxy", values, complex_table(length_y, 1.0))
    values = lax.all_to_all(values, "py", split_axis=4, concat_axis=2, tiled=True)
    values = swap_first(values)
    fields = einsum("fckxy,zck->fxyz", values, z_back)
    modulus = jnp.exp(0.5 * fields)
    levels = []
    level = modulus
    for _ in range(3):
        level = coarsen(level)
        levels.append(level)
    pieces = [jnp.reshape(level, (size_py, -1)) for level in levels]
    widths = [piece.shape[1] for piece in pieces]
    joined = jnp.concatenate(pieces, 1)
    spread = lax.all_to_all(joined, "py", split_axis=0, concat_axis=0, tiled=True)
    picked, start = ([], 0)
    for index, width in enumerate(widths):
        part = spread[:, start : start + width]
        picked.append(jnp.take(part, group_table[index], axis=0))
        start += width
    joined = lax.all_to_all(
        jnp.concatenate(picked, 1), "py", split_axis=0, concat_axis=0, tiled=True
    )
    routed, start = ([], 0)
    for level, width in zip(levels, widths):
        routed.append(joined[:, start : start + width].reshape(level.shape))
        start += width
    return (modulus, routed[0], routed[1], routed[2])


def solution(mesh):
    in_specs = (P(None, "px", "py", None), P("px", "py", None), P())
    out_specs = (P(None, "px", "py", None),) * 4
    return jax.shard_map(
        on_device, mesh=mesh, in_specs=in_specs, out_specs=out_specs, check_vma=False
    )
```

profile of v0, /device:TPU:0, one launch (start us, length us, event | category | flops | bytes accessed | tf_op | source)
XLA Modules:
  0.0 335.8 jit_solution(13237479351401507157)
XLA Ops:
  0.7 2.4 copy.69
  3.3 1.2 reshape.221
  4.5 6.4 %all-to-all-start.2 = ((f32[8,1,8704]{2,1,0:T(1,128)}), f32[8,1,8704]{2,1,0:T(1,128)S(1)}, u32[]{:S(2)}, u32[]{:S(2)}) async-start(f32[8,1,8704]{2,1,0:T(1,128)} %reshape.221), calls=%async_computation.2 | async-start | bytes 557056 | tf_op jit(solution)/shard_map/all_to_all | solution.py:58
  12.2 4.4 %copy.62 = f32[2,2,128,16,32]{4,3,0,1,2:T(8,128)} copy(f32[2,2,128,16,32]{2,4,3,0,1:T(8,128)S(1)} %pad_maximum_fusion.1) | data formatting | bytes 2097152 | tf_op jit(solution)/shard_map/concatenate | solution.py:38
  16.6 4.8 %reshape.219 = f32[8,1,32768]{2,1,0:T(1,128)} reshape(f32[128,2,2,16,32]{4,3,2,1,0:T(8,128)} %bitcast.161) | data formatting | bytes 2097152
  21.5 5.1 %all-to-all-start = ((f32[8,1,32768]{2,1,0:T(1,128)}), f32[8,1,32768]{2,1,0:T(1,128)S(1)}, u32[]{:S(2)}, u32[]{:S(2)}) async-start(f32[8,1,32768]{2,1,0:T(1,128)} %reshape.219), calls=%async_computation | async-start | bytes 2097152 | tf_op jit(solution)/shard_map/all_to_all | solution.py:67
  27.1 1.3 reduce.1
  28.8 0.6 copy.70
  29.9 0.8 pad_maximum_fusion.3
  30.7 22.5 %all-to-all-done = f32[8,1,32768]{2,1,0:T(1,128)S(1)} async-done(((f32[8,1,32768]{2,1,0:T(1,128)}), f32[8,1,32768]{2,1,0:T(1,128)S(1)}, u32[]{:S(2)}, u32[]{:S(2)}) %all-to-all-start) | async-done | bytes 1048608 | tf_op jit(solution)/shard_map/all_to_all | solution.py:67
  53.1 4.2 %all-to-all-start.3 = ((f32[4,5,16,256]{3,2,1,0:T(8,128)}), f32[4,5,16,256]{3,2,1,0:T(8,128)S(1)}, u32[]{:S(2)}, u32[]{:S(2)}) async-start(f32[4,5,16,256]{3,2,1,0:T(8,128)} %pad_maximum_fusion.3), calls=%async_computation.3 | async-start | bytes 655360 | tf_op jit(solution)/shard_map/all_to_all | solution.py:61
  57.3 3.1 reduce
  60.5 3.3 reshape.220
  63.8 6.6 %copy.64 = f32[2,2,16,16,8,32]{5,4,3,1,2,0:T(8,128)} copy(f32[2,2,16,16,8,32]{5,3,0,1,2,4:T(8,128)} %bitcast.162) | data formatting | bytes 2097152 | tf_op jit(solution)/shard_map/all_to_all | solution.py:67
  70.4 3.4 %reshape.204 = f32[2,2,16,16,256,1]{4,3,1,2,0,5:T(8,128)S(1)} reshape(f32[2,2,16,16,8,32]{5,4,3,1,2,0:T(8,128)} %copy.64) | data formatting | bytes 2097152 | tf_op jit(solution)/shard_map/all_to_all | solution.py:67
  73.9 1.0 convolution_bitcast_fusion.4
  74.9 1.0 copy.65
  76.0 4.3 %all-to-all-start.1 = ((f32[2,2,16,16,256]{4,3,1,0,2:T(8,128)}), f32[2,2,16,16,256]{4,3,1,0,2:T(8,128)S(1)}, u32[]{:S(2)}, u32[]{:S(2)}) async-start(f32[2,2,16,16,256]{4,3,1,0,2:T(8,128)} %copy.65), calls=%async_computation.1 | async-start | bytes 2097152 | tf_op jit(solution)/shard_map/all_to_all | solution.py:69
  80.5 12.5 %all-to-all-done.1 = f32[2,2,16,16,256]{4,3,1,0,2:T(8,128)S(1)} async-done(((f32[2,2,16,16,256]{4,3,1,0,2:T(8,128)}), f32[2,2,16,16,256]{4,3,1,0,2:T(8,128)S(1)}, u32[]{:S(2)}, u32[]{:S(2)}) %all-to-all-start.1) | async-done | bytes 1048608 | tf_op jit(solution)/shard_map/all_to_all | solution.py:69
  93.2 0.6 fusion.1
  93.8 0.6 convolution_bitcast_fusion.2
  94.4 0.8 copy.74
  95.3 16.1 %all_to_all.120 = f32[2,2,4,64,256]{4,1,2,0,3:T(2,128)S(1)} all-to-all(f32[2,2,4,64,256]{4,1,2,0,3:T(2,128)S(1)} %copy.74), channel_id=1, replica_groups=mesh['px'=4,'py'=8] {'px'}, dimensions={3} | all-to-all | bytes 2097152 | tf_op jit(solution)/shard_map/all_to_all | solution.py:73
  111.3 0.6 copy.75
  112.0 1.0 convolution_bitcast_fusion.1
  113.0 8.7 %copy.76 = f32[2,2,16,16,256]{3,1,2,0,4:T(2,128)} copy(f32[2,2,16,16,256]{4,3,1,2,0:T(8,128)S(1)} %convolution_bitcast_fusion.1) | data formatting | bytes 2097152 | tf_op jit(solution)/shard_map/fckxm,cmdy->fdkxy/transpose | solution.py:32
  121.7 13.6 %reshape.223 = f32[8,1,32768]{2,1,0:T(1,128)} reshape(f32[256,2,16,2,16]{4,3,2,1,0:T(2,128)} %bitcast.157) | data formatting | bytes 2097152
  135.3 3.7 %all-to-all-start.5 = ((f32[8,1,32768]{2,1,0:T(1,128)}), f32[8,1,32768]{2,1,0:T(1,128)S(1)}, u32[]{:S(2)}, u32[]{:S(2)}) async-start(f32[8,1,32768]{2,1,0:T(1,128)} %reshape.223), calls=%async_computation.5 | async-start | bytes 2097152 | tf_op jit(solution)/shard_map/all_to_all | solution.py:75
  139.0 26.4 %all-to-all-done.5 = f32[8,1,32768]{2,1,0:T(1,128)S(1)} async-done(((f32[8,1,32768]{2,1,0:T(1,128)}), f32[8,1,32768]{2,1,0:T(1,128)S(1)}, u32[]{:S(2)}, u32[]{:S(2)}) %all-to-all-start.5) | async-done | bytes 1048608 | tf_op jit(solution)/shard_map/all_to_all | solution.py:75
  165.5 3.1 reduce.2
  168.6 14.2 %reshape.224 = f32[256,2,16,2,16]{4,3,2,1,0:T(2,128)} reshape(f32[8,32768]{1,0:T(8,128)S(1)} %reduce.2) | data formatting | bytes 2097152
  182.9 12.9 %copy.77 = f32[2,2,16,16,8,32]{5,3,2,4,1,0:T(8,128)} copy(f32[2,2,16,16,8,32]{3,1,2,0,5,4:T(2,128)} %bitcast.158) | data formatting | bytes 2097152 | tf_op jit(solution)/shard_map/all_to_all | solution.py:75
  195.8 4.4 %slice.116 = f32[2,2,127,16,32]{4,3,2,1,0:T(8,128)} slice(f32[2,2,128,16,32]{4,3,2,1,0:T(8,128)} %bitcast.159), slice={[0:2], [0:2], [1:128], [0:16], [0:32]} | slice | bytes 2080768 | tf_op jit(solution)/shard_map/slice | solution.py:38
  200.2 0.8 slice.115
  201.0 3.8 %copy.104 = f32[2,2,127,16,32]{2,4,1,3,0:T(8,128)S(1)} copy(f32[2,2,127,16,32]{4,3,2,1,0:T(8,128)} %slice.116) | data formatting | bytes 2080768
  205.2 0.7 fusion.3
  206.0 68.4 %reshape.174 = f32[2,8,2,16,2,128,2]{6,5,4,3,2,1,0:T(8,128)} reshape(f32[2,16,32,256]{3,2,1,0:T(8,128)S(1)} %fusion.3) | data formatting | bytes 2097152 | tf_op jit(solution)/shard_map/reshape | solution.py:43
  274.3 20.8 %reduce_sum.27 = f32[2,8,16,128]{3,2,1,0:T(8,128)S(1)} reduce(f32[2,8,2,16,2,128,2]{6,5,4,3,2,1,0:T(8,128)} %reshape.174, f32[]{:T(128)} %constant.71.clone.1), dimensions={2,4,6}, to_apply=%region_0.1 | reduce | flops 229376 | bytes 1179652 | tf_op jit(solution)/shard_map/reduce_sum | solution.py:44
  295.1 9.8 %div.31 = f32[2,4,2,8,2,64,2]{6,5,4,3,2,1,0:T(8,128)} reshape(f32[2,8,16,128]{3,2,1,0:T(8,128)S(1)} %broadcast_multiply_fusion) | data formatting | bytes 262144 | tf_op jit(solution)/shard_map/div | solution.py:44
  304.9 4.1 %reduce_sum.28 = f32[2,4,8,64]{3,2,1,0:T(8,128)S(1)} reduce(f32[2,4,2,8,2,64,2]{6,5,4,3,2,1,0:T(8,128)} %div.31, f32[]{:T(128)} %constant.71.clone.1), dimensions={2,4,6}, to_apply=%region_1.2 | reduce | flops 28672 | bytes 147460 | tf_op jit(solution)/shard_map/reduce_sum | solution.py:44
  309.0 1.1 div.35
  310.5 0.8 all_to_all.106
  311.2 3.4 %all-to-all-start.6 = ((f32[8,1,4672]{2,1,0:T(1,128)}), f32[8,1,4672]{2,1,0:T(1,128)S(1)}, u32[]{:S(2)}, u32[]{:S(2)}) async-start(f32[8,1,4672]{2,1,0:T(1,128)} %all_to_all.106), calls=%async_computation.6 | async-start | bytes 303104 | tf_op jit(solution)/shard_map/all_to_all | solution.py:87
  314.6 6.9 %all-to-all-done.6 = f32[8,1,4672]{2,1,0:T(1,128)S(1)} async-done(((f32[8,1,4672]{2,1,0:T(1,128)}), f32[8,1,4672]{2,1,0:T(1,128)S(1)}, u32[]{:S(2)}, u32[]{:S(2)}) %all-to-all-start.6) | async-done | bytes 149536 | tf_op jit(solution)/shard_map/all_to_all | solution.py:87
  323.8 9.7 %all_to_all.121 = f32[8,1,4672]{2,1,0:T(1,128)S(1)} all-to-all(f32[8,1,4672]{2,1,0:T(1,128)S(1)} %copy.80), channel_id=1, replica_groups=mesh['px'=4,'py'=8] {'py'}, dimensions={0} | all-to-all | bytes 299008 | tf_op jit(solution)/shard_map/all_to_all | solution.py:93
  333.5 0.7 reshape.175
  334.2 0.7 reshape.176
  334.9 0.7 reshape.177
  (76 shorter events, 6.2 us)
Async XLA Ops:
  0.6 10.2 %copy-start = (f32[2,16,32,256]{3,2,1,0:T(8,128)S(1)}, f32[2,16,32,256]{3,2,1,0:T(8,128)}, u32[]{:S(2)}) copy-start(f32[2,16,32,256]{3,2,1,0:T(8,128)} %param.9) | copy-start | bytes 3145732
  0.6 10.2 %copy-start.5 = (f32[256,2,128,1,1]{2,0,4,3,1:T(8,128)S(1)}, f32[256,2,128,1,1]{2,0,4,3,1:T(8,128)}, u32[]{:S(2)}) copy-start(f32[256,2,128,1,1]{2,0,4,3,1:T(8,128)} %constant.80) | copy-start | bytes 786436
  4.5 17.0 %all-to-all-start.2 = ((f32[8,1,8704]{2,1,0:T(1,128)}), f32[8,1,8704]{2,1,0:T(1,128)S(1)}, u32[]{:S(2)}, u32[]{:S(2)}) async-start(f32[8,1,8704]{2,1,0:T(1,128)} %reshape.221), calls=%async_computation.2 | async-start | bytes 557056 | tf_op jit(solution)/shard_map/all_to_all | solution.py:58
  21.5 31.7 %all-to-all-start = ((f32[8,1,32768]{2,1,0:T(1,128)}), f32[8,1,32768]{2,1,0:T(1,128)S(1)}, u32[]{:S(2)}, u32[]{:S(2)}) async-start(f32[8,1,32768]{2,1,0:T(1,128)} %reshape.219), calls=%async_computation | async-start | bytes 2097152 | tf_op jit(solution)/shard_map/all_to_all | solution.py:67
  53.1 22.8 %all-to-all-start.3 = ((f32[4,5,16,256]{3,2,1,0:T(8,128)}), f32[4,5,16,256]{3,2,1,0:T(8,128)S(1)}, u32[]{:S(2)}, u32[]{:S(2)}) async-start(f32[4,5,16,256]{3,2,1,0:T(8,128)} %pad_maximum_fusion.3), calls=%async_computation.3 | async-start | bytes 655360 | tf_op jit(solution)/shard_map/all_to_all | solution.py:61
  70.4 3.4 %copy-start.4 = (f32[2,256,2,256,1,1]{3,1,0,2,5,4:T(8,128)S(1)}, f32[2,256,2,256,1,1]{3,1,0,2,5,4:T(8,128)}, u32[]{:S(2)}) copy-start(f32[2,256,2,256,1,1]{3,1,0,2,5,4:T(8,128)} %constant.81) | copy-start | bytes 3145732
  75.9 17.2 %copy-start.8 = (f32[2,64,2,64,1,1]{1,3,0,2,5,4:T(8,128)S(1)}, f32[2,64,2,64,1,1]{1,3,0,2,5,4:T(8,128)}, u32[]{:S(2)}) copy-start(f32[2,64,2,64,1,1]{1,3,0,2,5,4:T(8,128)} %constant.82) | copy-start | bytes 196612
  76.0 17.1 %all-to-all-start.1 = ((f32[2,2,16,16,256]{4,3,1,0,2:T(8,128)}), f32[2,2,16,16,256]{4,3,1,0,2:T(8,128)S(1)}, u32[]{:S(2)}, u32[]{:S(2)}) async-start(f32[2,2,16,16,256]{4,3,1,0,2:T(8,128)} %copy.65), calls=%async_computation.1 | async-start | bytes 2097152 | tf_op jit(solution)/shard_map/all_to_all | solution.py:69
  80.3 13.5 %copy-start.7 = (f32[2,64,2,64,1,1]{1,3,0,2,5,4:T(8,128)S(1)}, f32[2,64,2,64,1,1]{1,3,0,2,5,4:T(8,128)}, u32[]{:S(2)}) copy-start(f32[2,64,2,64,1,1]{1,3,0,2,5,4:T(8,128)} %constant.83) | copy-start | bytes 196612
  93.8 18.2 %copy-start.3 = (f32[2,256,2,256,1,1]{3,1,0,2,5,4:T(8,128)S(1)}, f32[2,256,2,256,1,1]{3,1,0,2,5,4:T(8,128)}, u32[]{:S(2)}) copy-start(f32[2,256,2,256,1,1]{3,1,0,2,5,4:T(8,128)} %constant.84) | copy-start | bytes 3145732
  121.7 17.3 %copy-start.9 = (s32[3,8]{1,0:T(4,128)S(1)}, s32[3,8]{1,0:T(4,128)}, u32[]{:S(2)}) copy-start(s32[3,8]{1,0:T(4,128)} %param.11) | copy-start | bytes 292
  135.3 30.2 %all-to-all-start.5 = ((f32[8,1,32768]{2,1,0:T(1,128)}), f32[8,1,32768]{2,1,0:T(1,128)S(1)}, u32[]{:S(2)}, u32[]{:S(2)}) async-start(f32[8,1,32768]{2,1,0:T(1,128)} %reshape.223), calls=%async_computation.5 | async-start | bytes 2097152 | tf_op jit(solution)/shard_map/all_to_all | solution.py:75
  200.2 5.1 %copy-start.6 = (f32[256,2,128,1,1]{2,0,1,4,3:T(8,128)S(1)}, f32[256,2,128,1,1]{2,0,1,4,3:T(8,128)}, u32[]{:S(2)}) copy-start(f32[256,2,128,1,1]{2,0,1,4,3:T(8,128)} %constant.85) | copy-start | bytes 786436
  206.0 68.4 %copy-start.2 = (f32[2,16,32,256]{3,2,1,0:T(8,128)}, f32[2,16,32,256]{3,2,1,0:T(8,128)S(1)}, u32[]{:S(2)}) copy-start(f32[2,16,32,256]{3,2,1,0:T(8,128)S(1)} %fusion.3) | copy-start | bytes 3145732
  304.9 30.6 %copy-start.1 = (f32[2,16,32,256]{3,2,1,0:T(8,128)S(1)}, f32[2,16,32,256]{3,2,1,0:T(8,128)}, u32[]{:S(2)}) copy-start(f32[2,16,32,256]{3,2,1,0:T(8,128)} %param.9) | copy-start | bytes 3145732
  311.2 10.3 %all-to-all-start.6 = ((f32[8,1,4672]{2,1,0:T(1,128)}), f32[8,1,4672]{2,1,0:T(1,128)S(1)}, u32[]{:S(2)}, u32[]{:S(2)}) async-start(f32[8,1,4672]{2,1,0:T(1,128)} %all_to_all.106), calls=%async_computation.6 | async-start | bytes 303104 | tf_op jit(solution)/shard_map/all_to_all | solution.py:87
where the time goes:
time: 342 us; the launch traced here: 336 us
  local copies, waits for them, and re-layouts  174 us (51%)
  waiting for transfers between devices  68.4 us (20%)
  other arithmetic  34.2 us (10%)
  starting transfers between devices  27.1 us (8%)
  blocking collectives  25.8 us (8%)
  matrix products  4.61 us (1%)
    reshape x1, local copies, waits for them, and re-layouts, coarsen(): values.reshape(members, size_x // 2, 2, size_y // 2, 2, size_z // 2, 2)  68.4 us
    unnamed x31, local copies, waits for them, and re-layouts  44.2 us
    all_to_all x1, waiting for transfers between devices, on_device(): lax.all_to_all(values, 'py', split_axis=4, concat_axis=2, tiled=True)  26.4 us
    reduce_sum x3, other arithmetic, coarsen(): return blocks.mean(axis=(2, 4, 6))  25 us
    all_to_all x1, waiting for transfers between devices, on_device(): lax.all_to_all(values, 'py', split_axis=2, concat_axis=4, tiled=True)  22.5 us
    all_to_all x1, blocking collectives, on_device(): lax.all_to_all(values, 'px', split_axis=3, concat_axis=2, tiled=True)  16.1 us
    all_to_all x1, local copies, waits for them, and re-layouts, on_device(): lax.all_to_all(values, 'py', split_axis=4, concat_axis=2, tiled=True)  12.9 us
    all_to_all x1, waiting for transfers between devices, on_device(): lax.all_to_all(values, 'px', split_axis=2, concat_axis=3, tiled=True)  12.5 us
  transfers between devices with their start and end apart: 6, of which 4 were waited for; matrix products, arithmetic and copies ran while one was open for 10% of the time, Pallas kernels for 0%

commit v1 on v0

--- a/solution.py
+++ b/solution.py
@@ -72,7 +72,11 @@
     values = einsum("fckjm,cjdx->fdkxm", values, complex_table(length_x, 1.0))
     values = lax.all_to_all(values, "px", split_axis=3, concat_axis=2, tiled=True)
     values = einsum("fckxm,cmdy->fdkxy", values, complex_table(length_y, 1.0))
-    values = lax.all_to_all(values, "py", split_axis=4, concat_axis=2, tiled=True)
+    shaped = jax.lax.axis_size("py")
+    all_rows = jnp.split(values, shaped, axis=4)
+    main = jnp.stack(all_rows, axis=0)
+    side_arr = jax.lax.all_to_all(main, "py", 0, 0)
+    values = jnp.concatenate(side_arr, axis=2)
     values = swap_first(values)
     fields = einsum("fckxy,zck->fxyz", values, z_back)
     modulus = jnp.exp(0.5 * fields)

time: 342 us -> 298 us (0.87); the launches traced: 336 us -> 297 us
  local copies, waits for them, and re-layouts: 174 us -> 137 us
    unnamed x31 -> x40, local copies, waits for them, and re-layouts: 44.2 us -> 27.4 us
    all_to_all x1 -> x0, local copies, waits for them, and re-layouts: 12.9 us -> none  [on_device(): lax.all_to_all(values, 'py', split_axis=4, concat_axis=2, tiled=True)]
    transpose x3 -> x2, local copies, waits for them, and re-layouts: 10.6 us -> 1.86 us  [einsum(): return jnp.einsum(pattern, left, right, precision=lax.Precision.HIGH)]
    reshape x0 -> x2, local copies, waits for them, and re-layouts: none -> 3.45 us  [on_device(): values = jnp.concatenate(side_arr, axis=2)]
  transfers between devices with their start and end apart: 6 -> 6, of which waited for: 4 -> 4; matrix products, arithmetic and copies ran while one was open for 10% -> 11% of each run, Pallas kernels for 0% -> 0%
where the time goes in v1:
time: 298 us; the launch traced here: 297 us
  local copies, waits for them, and re-layouts  137 us (46%)
  waiting for transfers between devices  68.2 us (23%)
  other arithmetic  34.2 us (11%)
  starting transfers between devices  26.6 us (9%)
  blocking collectives  25.7 us (9%)
  matrix products  4.61 us (2%)
    reshape x1, local copies, waits for them, and re-layouts, coarsen(): values.reshape(members, size_x // 2, 2, size_y // 2, 2, size_z // 2, 2)  68.4 us
    unnamed x40, local copies, waits for them, and re-layouts  27.4 us
    all_to_all x1, waiting for transfers between devices, on_device(): side_arr = jax.lax.all_to_all(main, 'py', 0, 0)  26.2 us
    reduce_sum x3, other arithmetic, coarsen(): return blocks.mean(axis=(2, 4, 6))  25 us
    all_to_all x1, waiting for transfers between devices, on_device(): lax.all_to_all(values, 'py', split_axis=2, concat_axis=4, tiled=True)  22.4 us
    all_to_all x1, blocking collectives, on_device(): lax.all_to_all(values, 'px', split_axis=3, concat_axis=2, tiled=True)  16.1 us
    all_to_all x1, waiting for transfers between devices, on_device(): lax.all_to_all(values, 'px', split_axis=2, concat_axis=3, tiled=True)  12.6 us
    div x5, local copies, waits for them, and re-layouts, coarsen(): return blocks.mean(axis=(2, 4, 6))  11 us
  transfers between devices with their start and end apart: 6, of which 4 were waited for; matrix products, arithmetic and copies ran while one was open for 11% of the time, Pallas kernels for 0%

profile of v1, /device:TPU:0, one launch (start us, length us, event | category | flops | bytes accessed | tf_op | source)
XLA Modules:
  0.0 297.4 jit_solution(13409496772535651168)
XLA Ops:
  0.7 2.4 copy.67
  3.3 1.2 reshape.229
  4.5 6.4 %all-to-all-start.2 = ((f32[8,1,8704]{2,1,0:T(1,128)}), f32[8,1,8704]{2,1,0:T(1,128)S(1)}, u32[]{:S(2)}, u32[]{:S(2)}) async-start(f32[8,1,8704]{2,1,0:T(1,128)} %reshape.229), calls=%async_computation.2 | async-start | bytes 557056 | tf_op jit(solution)/shard_map/all_to_all | solution.py:58
  12.2 4.4 %copy.60 = f32[2,2,128,16,32]{4,3,0,1,2:T(8,128)} copy(f32[2,2,128,16,32]{2,4,3,0,1:T(8,128)S(1)} %pad_maximum_fusion.1) | data formatting | bytes 2097152 | tf_op jit(solution)/shard_map/concatenate | solution.py:38
  16.6 4.8 %reshape.227 = f32[8,1,32768]{2,1,0:T(1,128)} reshape(f32[128,2,2,16,32]{4,3,2,1,0:T(8,128)} %bitcast.189) | data formatting | bytes 2097152
  21.5 5.1 %all-to-all-start = ((f32[8,1,32768]{2,1,0:T(1,128)}), f32[8,1,32768]{2,1,0:T(1,128)S(1)}, u32[]{:S(2)}, u32[]{:S(2)}) async-start(f32[8,1,32768]{2,1,0:T(1,128)} %reshape.227), calls=%async_computation | async-start | bytes 2097152 | tf_op jit(solution)/shard_map/all_to_all | solution.py:67
  27.1 1.3 reduce.1
  28.8 0.6 copy.68
  29.9 0.8 pad_maximum_fusion.3
  30.7 22.4 %all-to-all-done = f32[8,1,32768]{2,1,0:T(1,128)S(1)} async-done(((f32[8,1,32768]{2,1,0:T(1,128)}), f32[8,1,32768]{2,1,0:T(1,128)S(1)}, u32[]{:S(2)}, u32[]{:S(2)}) %all-to-all-start) | async-done | bytes 1048608 | tf_op jit(solution)/shard_map/all_to_all | solution.py:67
  53.1 3.7 %all-to-all-start.3 = ((f32[4,5,16,256]{3,2,1,0:T(8,128)}), f32[4,5,16,256]{3,2,1,0:T(8,128)S(1)}, u32[]{:S(2)}, u32[]{:S(2)}) async-start(f32[4,5,16,256]{3,2,1,0:T(8,128)} %pad_maximum_fusion.3), calls=%async_computation.3 | async-start | bytes 655360 | tf_op jit(solution)/shard_map/all_to_all | solution.py:61
  56.9 3.1 %reduce = f32[8,32768]{1,0:T(8,128)S(1)} reduce(f32[8,1,32768]{2,1,0:T(1,128)S(1)} %all-to-all-done, f32[]{:T(128)} %broadcast.137), dimensions={1}, to_apply=%all_to_all.76.reduce_sub_computation | reduce | bytes 2097156 | tf_op jit(solution)/shard_map/all_to_all | solution.py:67
  60.0 3.3 %reshape.228 = f32[128,2,2,16,32]{4,3,2,1,0:T(8,128)} reshape(f32[8,32768]{1,0:T(8,128)S(1)} %reduce) | data formatting | bytes 2097152
  63.3 6.6 %copy.62 = f32[2,2,16,16,8,32]{5,4,3,1,2,0:T(8,128)} copy(f32[2,2,16,16,8,32]{5,3,0,1,2,4:T(8,128)} %bitcast.190) | data formatting | bytes 2097152 | tf_op jit(solution)/shard_map/all_to_all | solution.py:67
  69.9 3.4 %reshape.212 = f32[2,2,16,16,256,1]{4,3,1,2,0,5:T(8,128)S(1)} reshape(f32[2,2,16,16,8,32]{5,4,3,1,2,0:T(8,128)} %copy.62) | data formatting | bytes 2097152 | tf_op jit(solution)/shard_map/all_to_all | solution.py:67
  73.4 1.0 convolution_bitcast_fusion.4
  74.4 1.0 copy.63
  75.5 4.3 %all-to-all-start.1 = ((f32[2,2,16,16,256]{4,3,1,0,2:T(8,128)}), f32[2,2,16,16,256]{4,3,1,0,2:T(8,128)S(1)}, u32[]{:S(2)}, u32[]{:S(2)}) async-start(f32[2,2,16,16,256]{4,3,1,0,2:T(8,128)} %copy.63), calls=%async_computation.1 | async-start | bytes 2097152 | tf_op jit(solution)/shard_map/all_to_all | solution.py:69
  80.0 12.6 %all-to-all-done.1 = f32[2,2,16,16,256]{4,3,1,0,2:T(8,128)S(1)} async-done(((f32[2,2,16,16,256]{4,3,1,0,2:T(8,128)}), f32[2,2,16,16,256]{4,3,1,0,2:T(8,128)S(1)}, u32[]{:S(2)}, u32[]{:S(2)}) %all-to-all-start.1) | async-done | bytes 1048608 | tf_op jit(solution)/shard_map/all_to_all | solution.py:69
  92.7 0.6 fusion.1
  93.4 0.6 convolution_bitcast_fusion.2
  94.0 0.8 copy.72
  94.8 16.1 %all_to_all.107 = f32[2,2,4,64,256]{4,1,2,0,3:T(2,128)S(1)} all-to-all(f32[2,2,4,64,256]{4,1,2,0,3:T(2,128)S(1)} %copy.72), channel_id=1, replica_groups=mesh['px'=4,'py'=8] {'px'}, dimensions={3} | all-to-all | bytes 2097152 | tf_op jit(solution)/shard_map/all_to_all | solution.py:73
  110.9 0.6 copy.73
  111.5 1.0 convolution_bitcast_fusion.1
  113.9 1.9 copy-done.2
  115.8 4.8 %reshape.231 = f32[8,1,32768]{2,1,0:T(1,128)} reshape(f32[8,2,16,2,16,32]{5,4,3,2,1,0:T(8,128)} %bitcast.193) | data formatting | bytes 2097152
  120.7 3.8 %all-to-all-start.5 = ((f32[8,1,32768]{2,1,0:T(1,128)}), f32[8,1,32768]{2,1,0:T(1,128)S(1)}, u32[]{:S(2)}, u32[]{:S(2)}) async-start(f32[8,1,32768]{2,1,0:T(1,128)} %reshape.231), calls=%async_computation.5 | async-start | bytes 2097152 | tf_op jit(solution)/shard_map/all_to_all | solution.py:78
  124.5 26.2 %all-to-all-done.5 = f32[8,1,32768]{2,1,0:T(1,128)S(1)} async-done(((f32[8,1,32768]{2,1,0:T(1,128)}), f32[8,1,32768]{2,1,0:T(1,128)S(1)}, u32[]{:S(2)}, u32[]{:S(2)}) %all-to-all-start.5) | async-done | bytes 1048608 | tf_op jit(solution)/shard_map/all_to_all | solution.py:78
  150.7 3.1 %reduce.2 = f32[8,32768]{1,0:T(8,128)S(1)} reduce(f32[8,1,32768]{2,1,0:T(1,128)S(1)} %all-to-all-done.5, f32[]{:T(128)} %broadcast.137), dimensions={1}, to_apply=%all_to_all.92.reduce_sub_computation | reduce | bytes 2097156 | tf_op jit(solution)/shard_map/all_to_all | solution.py:78
  153.9 3.3 %reshape.232 = f32[8,2,16,2,16,32]{5,4,3,2,1,0:T(8,128)} reshape(f32[8,32768]{1,0:T(8,128)S(1)} %reduce.2) | data formatting | bytes 2097152
  157.2 2.9 bitcast_bitcast_fusion
  160.7 2.3 slice.116
  163.0 3.6 %copy.101 = f32[2,2,127,16,32]{2,4,1,3,0:T(8,128)S(1)} copy(f32[2,2,127,16,32]{4,3,2,1,0:T(8,128)} %slice.116) | data formatting | bytes 2080768
  167.1 0.7 fusion.3
  167.9 68.4 %reshape.182 = f32[2,8,2,16,2,128,2]{6,5,4,3,2,1,0:T(8,128)} reshape(f32[2,16,32,256]{3,2,1,0:T(8,128)S(1)} %fusion.3) | data formatting | bytes 2097152 | tf_op jit(solution)/shard_map/reshape | solution.py:43
  236.2 20.8 %reduce_sum.27 = f32[2,8,16,128]{3,2,1,0:T(8,128)S(1)} reduce(f32[2,8,2,16,2,128,2]{6,5,4,3,2,1,0:T(8,128)} %reshape.182, f32[]{:T(128)} %constant.71.clone.1), dimensions={2,4,6}, to_apply=%region_0.1 | reduce | flops 229376 | bytes 1179652 | tf_op jit(solution)/shard_map/reduce_sum | solution.py:44
  257.0 9.8 %div.31 = f32[2,4,2,8,2,64,2]{6,5,4,3,2,1,0:T(8,128)} reshape(f32[2,8,16,128]{3,2,1,0:T(8,128)S(1)} %broadcast_multiply_fusion) | data formatting | bytes 262144 | tf_op jit(solution)/shard_map/div | solution.py:44
  266.8 4.1 %reduce_sum.28 = f32[2,4,8,64]{3,2,1,0:T(8,128)S(1)} reduce(f32[2,4,2,8,2,64,2]{6,5,4,3,2,1,0:T(8,128)} %div.31, f32[]{:T(128)} %constant.71.clone.1), dimensions={2,4,6}, to_apply=%region_1.2 | reduce | flops 28672 | bytes 147460 | tf_op jit(solution)/shard_map/reduce_sum | solution.py:44
  270.9 1.1 div.35
  272.4 0.8 all_to_all.93
  273.1 3.4 %all-to-all-start.6 = ((f32[8,1,4672]{2,1,0:T(1,128)}), f32[8,1,4672]{2,1,0:T(1,128)S(1)}, u32[]{:S(2)}, u32[]{:S(2)}) async-start(f32[8,1,4672]{2,1,0:T(1,128)} %all_to_all.93), calls=%async_computation.6 | async-start | bytes 303104 | tf_op jit(solution)/shard_map/all_to_all | solution.py:91
  276.5 6.9 %all-to-all-done.6 = f32[8,1,4672]{2,1,0:T(1,128)S(1)} async-done(((f32[8,1,4672]{2,1,0:T(1,128)}), f32[8,1,4672]{2,1,0:T(1,128)S(1)}, u32[]{:S(2)}, u32[]{:S(2)}) %all-to-all-start.6) | async-done | bytes 149536 | tf_op jit(solution)/shard_map/all_to_all | solution.py:91
  283.5 0.6 gather_fusion
  285.7 9.7 %all_to_all.108 = f32[8,1,4672]{2,1,0:T(1,128)S(1)} all-to-all(f32[8,1,4672]{2,1,0:T(1,128)S(1)} %copy.77), channel_id=1, replica_groups=mesh['px'=4,'py'=8] {'py'}, dimensions={0} | all-to-all | bytes 299008 | tf_op jit(solution)/shard_map/all_to_all | solution.py:97
  295.4 0.7 reshape.183
  296.1 0.7 reshape.184
  296.8 0.7 reshape.185
  (86 shorter events, 7.5 us)
Async XLA Ops:
  0.6 10.2 %copy-start = (f32[2,16,32,256]{3,2,1,0:T(8,128)S(1)}, f32[2,16,32,256]{3,2,1,0:T(8,128)}, u32[]{:S(2)}) copy-start(f32[2,16,32,256]{3,2,1,0:T(8,128)} %param.9) | copy-start | bytes 3145732
  0.6 10.2 %copy-start.6 = (f32[256,2,128,1,1]{2,0,4,3,1:T(8,128)S(1)}, f32[256,2,128,1,1]{2,0,4,3,1:T(8,128)}, u32[]{:S(2)}) copy-start(f32[256,2,128,1,1]{2,0,4,3,1:T(8,128)} %constant.80) | copy-start | bytes 786436
  4.5 17.0 %all-to-all-start.2 = ((f32[8,1,8704]{2,1,0:T(1,128)}), f32[8,1,8704]{2,1,0:T(1,128)S(1)}, u32[]{:S(2)}, u32[]{:S(2)}) async-start(f32[8,1,8704]{2,1,0:T(1,128)} %reshape.229), calls=%async_computation.2 | async-start | bytes 557056 | tf_op jit(solution)/shard_map/all_to_all | solution.py:58
  21.5 31.7 %all-to-all-start = ((f32[8,1,32768]{2,1,0:T(1,128)}), f32[8,1,32768]{2,1,0:T(1,128)S(1)}, u32[]{:S(2)}, u32[]{:S(2)}) async-start(f32[8,1,32768]{2,1,0:T(1,128)} %reshape.227), calls=%async_computation | async-start | bytes 2097152 | tf_op jit(solution)/shard_map/all_to_all | solution.py:67
  53.1 22.3 %all-to-all-start.3 = ((f32[4,5,16,256]{3,2,1,0:T(8,128)}), f32[4,5,16,256]{3,2,1,0:T(8,128)S(1)}, u32[]{:S(2)}, u32[]{:S(2)}) async-start(f32[4,5,16,256]{3,2,1,0:T(8,128)} %pad_maximum_fusion.3), calls=%async_computation.3 | async-start | bytes 655360 | tf_op jit(solution)/shard_map/all_to_all | solution.py:61
  69.9 3.4 %copy-start.5 = (f32[2,256,2,256,1,1]{3,1,0,2,5,4:T(8,128)S(1)}, f32[2,256,2,256,1,1]{3,1,0,2,5,4:T(8,128)}, u32[]{:S(2)}) copy-start(f32[2,256,2,256,1,1]{3,1,0,2,5,4:T(8,128)} %constant.81) | copy-start | bytes 3145732
  75.5 17.3 %copy-start.9 = (f32[2,64,2,64,1,1]{1,3,0,2,5,4:T(8,128)S(1)}, f32[2,64,2,64,1,1]{1,3,0,2,5,4:T(8,128)}, u32[]{:S(2)}) copy-start(f32[2,64,2,64,1,1]{1,3,0,2,5,4:T(8,128)} %constant.82) | copy-start | bytes 196612
  75.5 17.2 %all-to-all-start.1 = ((f32[2,2,16,16,256]{4,3,1,0,2:T(8,128)}), f32[2,2,16,16,256]{4,3,1,0,2:T(8,128)S(1)}, u32[]{:S(2)}, u32[]{:S(2)}) async-start(f32[2,2,16,16,256]{4,3,1,0,2:T(8,128)} %copy.63), calls=%async_computation.1 | async-start | bytes 2097152 | tf_op jit(solution)/shard_map/all_to_all | solution.py:69
  79.8 13.6 %copy-start.8 = (f32[2,64,2,64,1,1]{1,3,0,2,5,4:T(8,128)S(1)}, f32[2,64,2,64,1,1]{1,3,0,2,5,4:T(8,128)}, u32[]{:S(2)}) copy-start(f32[2,64,2,64,1,1]{1,3,0,2,5,4:T(8,128)} %constant.83) | copy-start | bytes 196612
  93.4 18.1 %copy-start.4 = (f32[2,256,2,256,1,1]{3,1,0,2,5,4:T(8,128)S(1)}, f32[2,256,2,256,1,1]{3,1,0,2,5,4:T(8,128)}, u32[]{:S(2)}) copy-start(f32[2,256,2,256,1,1]{3,1,0,2,5,4:T(8,128)} %constant.84) | copy-start | bytes 3145732
  113.7 10.8 %copy-start.10 = (s32[3,8]{1,0:T(4,128)S(1)}, s32[3,8]{1,0:T(4,128)}, u32[]{:S(2)}) copy-start(s32[3,8]{1,0:T(4,128)} %param.11) | copy-start | bytes 292
  113.9 1.9 copy-start.2
  120.7 30.1 %all-to-all-start.5 = ((f32[8,1,32768]{2,1,0:T(1,128)}), f32[8,1,32768]{2,1,0:T(1,128)S(1)}, u32[]{:S(2)}, u32[]{:S(2)}) async-start(f32[8,1,32768]{2,1,0:T(1,128)} %reshape.231), calls=%async_computation.5 | async-start | bytes 2097152 | tf_op jit(solution)/shard_map/all_to_all | solution.py:78
  163.0 4.1 %copy-start.7 = (f32[256,2,128,1,1]{2,0,1,4,3:T(8,128)S(1)}, f32[256,2,128,1,1]{2,0,1,4,3:T(8,128)}, u32[]{:S(2)}) copy-start(f32[256,2,128,1,1]{2,0,1,4,3:T(8,128)} %constant.85) | copy-start | bytes 786436
  167.8 68.4 %copy-start.3 = (f32[2,16,32,256]{3,2,1,0:T(8,128)}, f32[2,16,32,256]{3,2,1,0:T(8,128)S(1)}, u32[]{:S(2)}) copy-start(f32[2,16,32,256]{3,2,1,0:T(8,128)S(1)} %fusion.3) | copy-start | bytes 3145732
  266.8 30.6 %copy-start.1 = (f32[2,16,32,256]{3,2,1,0:T(8,128)S(1)}, f32[2,16,32,256]{3,2,1,0:T(8,128)}, u32[]{:S(2)}) copy-start(f32[2,16,32,256]{3,2,1,0:T(8,128)} %param.9) | copy-start | bytes 3145732
  273.1 10.3 %all-to-all-start.6 = ((f32[8,1,4672]{2,1,0:T(1,128)}), f32[8,1,4672]{2,1,0:T(1,128)S(1)}, u32[]{:S(2)}, u32[]{:S(2)}) async-start(f32[8,1,4672]{2,1,0:T(1,128)} %all_to_all.93), calls=%async_computation.6 | async-start | bytes 303104 | tf_op jit(solution)/shard_map/all_to_all | solution.py:91
